TPU v7x, 1024 devices: a whole 8x8x8 slice. The times are simulated.
1024 devices in a mesh: row: 16 (over y, core), col: 64 (over z, x).
Axes of the slice: x: 8, y: 8, z: 8, core: 2. Of those that a mesh axis runs over, the one named last changes fastest.
Arguments:
- tokens: bfloat16 [320, 8192], P('col', 'row'), may hold values from -6 to 6
- grad_out: bfloat16 [320, 8192], P('col', 'row'), may hold values from -6 to 6
- gate_weight: bfloat16 [8192, 28672], P('row', 'col'), may hold values from -0.0625 to 0.0625
- up_weight: bfloat16 [8192, 28672], P('row', 'col'), may hold values from -0.0625 to 0.0625
- down_weight: bfloat16 [28672, 8192], P('col', 'row'), may hold values from -0.03125 to 0.03125
Outputs:
- grad_tokens: bfloat16 [320, 8192], P('col', 'row')
- grad_gate_weight: bfloat16 [8192, 28672], P('row', 'col')
- grad_up_weight: bfloat16 [8192, 28672], P('row', 'col')
- grad_down_weight: bfloat16 [28672, 8192], P('col', 'row')
All inputs are finite; a program needn't handle non-finite values.
Results may differ from a plain program's by a relative error of at most 0.0049.
Values may be sent and summed in bfloat16 or wider, within the bound.
A program may use at most 32 MiB of HBM per device.

v0:
```python
import jax
import jax.numpy as jnp
from jax import lax
from jax.sharding import PartitionSpec as P


def in_one_piece(arrays, axis, dim, along):
    widths = [a.shape[along] for a in arrays]
    both = jnp.concatenate(arrays, axis=along)
    out = lax.all_gather(both, axis, axis=dim, tiled=True)
    return tuple(jnp.split(out, [sum(widths[:k]) for k in range(1, len(widths))], axis=along))


def cut_along(shard, dim, length):
    lengths = shard.shape
    tiles = shard.reshape(*lengths[:dim], length, lengths[dim] // length, *lengths[dim + 1 :])
    return jnp.moveaxis(tiles, dim, 0)


def sent_and_summed(shard, axis, dim):
    length = lax.axis_size(axis)
    tiles = lax.all_to_all(cut_along(shard, dim, length), axis, 0, 0, tiled=True)
    return jnp.sum(tiles, axis=0)


def hidden_grads(gate_sum, up_sum, back_sum):
    sigmoid_gate = 1.0 / (1.0 + jnp.exp(-gate_sum))
    activated = gate_sum * sigmoid_gate
    hidden = (activated * up_sum).astype(jnp.bfloat16)
    grad_up = (back_sum * activated).astype(jnp.bfloat16)
    slope = sigmoid_gate * (1.0 + gate_sum * (1.0 - sigmoid_gate))
    grad_gate = (back_sum * up_sum * slope).astype(jnp.bfloat16)
    return (hidden, grad_gate, grad_up)


def shards(tokens, grad_out, gate_weight, up_weight, down_weight):
    tok_full, grad_full = in_one_piece((tokens, grad_out), "col", 0, 1)
    hidden_width = gate_weight.shape[1]
    gate_part = jnp.dot(tok_full, gate_weight, preferred_element_type=jnp.float32)
    up_part = jnp.dot(tok_full, up_weight, preferred_element_type=jnp.float32)
    back_part = jnp.einsum("td,fd->tf", grad_full, down_weight, preferred_element_type=jnp.float32)
    sums = sent_and_summed(jnp.concatenate([gate_part, up_part, back_part], axis=1), "row", 0)
    hidden_local, gate_local, up_local = hidden_grads(
        sums[:, :hidden_width],
        sums[:, hidden_width : 2 * hidden_width],
        sums[:, 2 * hidden_width :],
    )
    hidden, grad_gate, grad_up = in_one_piece((hidden_local, gate_local, up_local), "row", 0, 1)
    grad_down_weight = jnp.einsum(
        "tf,td->fd", hidden, grad_full, preferred_element_type=jnp.float32
    ).astype(jnp.bfloat16)
    grad_gate_weight = jnp.einsum(
        "td,tf->df", tok_full, grad_gate, preferred_element_type=jnp.float32
    ).astype(jnp.bfloat16)
    grad_up_weight = jnp.einsum(
        "td,tf->df", tok_full, grad_up, preferred_element_type=jnp.float32
    ).astype(jnp.bfloat16)
    total = jnp.einsum("tf,df->td", grad_gate, gate_weight, preferred_element_type=jnp.float32)
    grad_tokens = sent_and_summed(
        total + jnp.einsum("tf,df->td", grad_up, up_weight, preferred_element_type=jnp.float32),
        "col",
        0,
    ).astype(jnp.bfloat16)
    return (grad_tokens, grad_gate_weight, grad_up_weight, grad_down_weight)


def solution(mesh):
    placed = (P("col", "row"), P("col", "row"), P("row", "col"), P("row", "col"), P("col", "row"))
    return jax.shard_map(
        shards,
        mesh=mesh,
        in_specs=placed,
        out_specs=(P("col", "row"), P("row", "col"), P("row", "col"), P("col", "row")),
        check_vma=False,
    )
```

profile of v0, /device:TPU:6, one launch (start us, length us, event | category | flops | bytes accessed | tf_op | source)
XLA Modules:
  0.0 189.7 jit_solution(2270839966995720495)
XLA Ops:
  0.6 0.0 copy-start
  0.6 0.0 copy-start.1
  0.7 0.0 copy-start.3
  0.7 0.8 maximum_bitcast_fusion
  1.5 62.1 %all-gather = bf16[64,5,1024]{2,1,0:T(8,128)(2,1)S(1)} all-gather(bf16[1,5,1024]{2,1,0:T(8,128)(2,1)S(1)} %maximum_bitcast_fusion), channel_id=1, replica_groups=mesh['row'=16,'col'=64] {'col'}, dimensions={0}, use_global_device_ids=true | all-gather | bytes 665600 | tf_op jit(solution)/shard_map/all_gather | solution.py:10
  63.6 0.3 reshape.17
  63.9 0.0 copy-done.1
  63.9 0.4 fusion.11
  64.3 0.0 copy-done.3
  64.3 0.4 fusion.7
  64.6 0.0 copy-done
  64.6 0.4 fusion.13
  65.0 1.6 concatenate.10
  66.6 1.5 reshape.14
  68.1 60.2 %all_to_all.10 = f32[16,20,1344]{2,1,0:T(8,128)} all-to-all(f32[16,20,1344]{2,1,0:T(8,128)S(1)} %reshape.14), channel_id=1, replica_groups=mesh['row'=16,'col'=64] {'row'}, dimensions={0} | all-to-all | bytes 3440640 | tf_op jit(solution)/shard_map/all_to_all | solution.py:22
  128.3 1.7 reduce_sum.18
  130.0 0.1 multiply_convert_fusion
  130.1 0.1 concatenate.11
  130.2 0.0 copy-start.2
  130.2 18.1 %all-gather.1 = bf16[16,20,1344]{2,1,0:T(8,128)(2,1)S(1)} all-gather(bf16[1,20,1344]{2,1,0:T(8,128)(2,1)S(1)} %bitcast.8), channel_id=1, replica_groups=mesh['row'=16,'col'=64] {'row'}, dimensions={0}, use_global_device_ids=true | all-gather | bytes 913920 | tf_op jit(solution)/shard_map/all_gather | solution.py:10
  148.4 0.4 reshape.19
  148.8 0.4 fusion.4
  149.2 0.0 copy-done.2
  149.2 0.3 convolution_add_fusion
  149.5 1.1 reshape.15
  150.6 8.6 %all-to-all-start.1 = ((f32[64,5,512]{2,1,0:T(8,128)}), f32[64,5,512]{2,1,0:T(8,128)S(1)}, u32[]{:S(2)}, u32[]{:S(2)}) async-start(f32[64,5,512]{2,1,0:T(8,128)} %reshape.15), calls=%async_computation.1 | async-start | bytes 2097152 | tf_op jit(solution)/shard_map/all_to_all | solution.py:22
  159.2 1.5 convolution_convert_fusion.2
  160.7 1.2 convolution_convert_fusion.1
  161.9 1.2 convolution_convert_fusion
  163.1 25.9 %all-to-all-done.1 = f32[64,5,512]{2,1,0:T(8,128)S(1)} async-done(((f32[64,5,512]{2,1,0:T(8,128)}), f32[64,5,512]{2,1,0:T(8,128)S(1)}, u32[]{:S(2)}, u32[]{:S(2)}) %all-to-all-start.1) | async-done | bytes 655392 | tf_op jit(solution)/shard_map/all_to_all | solution.py:22
  189.0 0.7 reduce_sum.19
Async XLA Ops:
  0.6 64.0 %copy-start = (bf16[512,448]{0,1:T(8,128)(2,1)S(1)}, bf16[512,448]{0,1:T(8,128)(2,1)}, u32[]{:S(2)}) copy-start(bf16[512,448]{0,1:T(8,128)(2,1)} %param.7) | copy-start | bytes 1376260
  0.6 63.3 %copy-start.1 = (bf16[512,448]{0,1:T(8,128)(2,1)S(1)}, bf16[512,448]{0,1:T(8,128)(2,1)}, u32[]{:S(2)}) copy-start(bf16[512,448]{0,1:T(8,128)(2,1)} %param.8) | copy-start | bytes 1376260
  0.7 63.6 %copy-start.3 = (bf16[448,512]{1,0:T(8,128)(2,1)S(1)}, bf16[448,512]{1,0:T(8,128)(2,1)}, u32[]{:S(2)}) copy-start(bf16[448,512]{1,0:T(8,128)(2,1)} %param.9) | copy-start | bytes 1376260
  130.2 18.9 %copy-start.2 = (bf16[512,448]{0,1:T(8,128)(2,1)S(1)}, bf16[512,448]{0,1:T(8,128)(2,1)}, u32[]{:S(2)}) copy-start(bf16[512,448]{0,1:T(8,128)(2,1)} %param.8) | copy-start | bytes 1376260
  150.6 38.4 %all-to-all-start.1 = ((f32[64,5,512]{2,1,0:T(8,128)}), f32[64,5,512]{2,1,0:T(8,128)S(1)}, u32[]{:S(2)}, u32[]{:S(2)}) async-start(f32[64,5,512]{2,1,0:T(8,128)} %reshape.15), calls=%async_computation.1 | async-start | bytes 2097152 | tf_op jit(solution)/shard_map/all_to_all | solution.py:22
where the time goes:
time: 190 us
  blocking collectives  140 us (74%)
  waiting for transfers between devices  25.9 us (14%)
  starting transfers between devices  8.62 us (5%)
  matrix products  5.65 us (3%)
  local copies, waits for them, and re-layouts  4.95 us (3%)
  other arithmetic  3.34 us (2%)
    all_gather x2, blocking collectives, in_one_piece(): out = lax.all_gather(both, axis, axis=dim, tiled=True)  80.3 us
    all_to_all x1, blocking collectives, sent_and_summed(): lax.all_to_all(cut_along(shard, dim, length), axis, 0, 0, tiled=True)  60.2 us
    all_to_all x1, waiting for transfers between devices, sent_and_summed(): lax.all_to_all(cut_along(shard, dim, length), axis, 0, 0, tiled=True)  25.9 us
    all_to_all x1, starting transfers between devices, sent_and_summed(): lax.all_to_all(cut_along(shard, dim, length), axis, 0, 0, tiled=True)  8.62 us
  transfers between devices with their start and end apart: 1, of which 1 were waited for; matrix products, arithmetic and copies ran while one was open for 2% of the time, Pallas kernels for 0%

commit v1 on v0

v1 whole, which is shorter than its diff:
```python
import functools

import jax
import jax.numpy as jnp
from jax import lax
from jax.experimental import pallas as pl
from jax.experimental.pallas import tpu as pltpu
from jax.sharding import PartitionSpec as P

MESH = pl.DeviceIdType.MESH
BF16 = jnp.bfloat16
F32 = jnp.float32
PAD = 8


def near_first(n):
    order = []
    for k in range(1, n // 2 + 1):
        order.append(k)
        if n - k != k:
            order.append(n - k)
    return order


def across(a, b):
    return lax.dot_general(a, b, (((1,), (1,)), ((), ())), preferred_element_type=F32)


def down(a, b):
    return lax.dot_general(a, b, (((0,), (0,)), ((), ())), preferred_element_type=F32)


def plain(a, b):
    return lax.dot_general(a, b, (((1,), (0,)), ((), ())), preferred_element_type=F32)


def kernel(
    n, nx,
    tok_ref, grad_ref, wg_ref, wu_ref, wd_ref,
    gtok_ref, gg_out, gu_out, gd_out,
    tok_in, grad_in, w_all, tok1, grad1, tok_full, grad_x, grad_full,
    pair_src, pair_dst, own_sum, y_src, y_dst,
    back, back_dst, own_back, yb_src, yb_dst,
    hid, d_dst, d_src, e_src, e_dst,
    load_sem, s_tok1, r_tok1, s_grad1, r_grad1, s_tok2, r_tok2, s_grad2, r_grad2,
    s_pair, r_pair, s_y, r_y, s_pairb, r_pairb, s_yb, r_yb, s_hid, r_hid, s_fwd, s_d, r_d, s_e, r_e,
):
    rows, width = tok_ref.shape
    group = rows * nx
    hidden = wd_ref.shape[0]
    two = 2 * hidden
    half = n // 2

    row, col = lax.axis_index("row"), lax.axis_index("col")
    y, core = lax.div(row, 2), lax.rem(row, 2)
    z, x = lax.div(col, nx), lax.rem(col, nx)
    other = row + 1 - 2 * core

    def at_x(k):
        return (row, z * nx + k)

    def at_z(k):
        return (row, k * nx + x)

    def at_y(k):
        return (2 * k + core, col)

    pair = (other, col)

    def send(src, dst, s, r, device):
        return pltpu.make_async_remote_copy(
            src_ref=src, dst_ref=dst, send_sem=s, recv_sem=r, device_id=device, device_id_type=MESH
        )

    def step(a, k, m):
        return lax.rem(a + k, m)

    def mine(g):
        k = lax.rem(z - g + n, n)
        return core == jnp.where((k >= 1) & (k <= half), 1, 0)

    def kept(m, who):
        k = who * (m + 1) + (1 - who) * ((n - m) % n)
        return lax.rem(z - k + 2 * n, n)

    loads = [
        pltpu.make_async_copy(wg_ref, w_all.at[pl.ds(0, hidden)], load_sem.at[0]),
        pltpu.make_async_copy(wu_ref, w_all.at[pl.ds(hidden, hidden)], load_sem.at[1]),
        pltpu.make_async_copy(wd_ref, w_all.at[pl.ds(two, hidden)], load_sem.at[2]),
    ]
    fetches = [
        pltpu.make_async_copy(tok_ref, tok_in, load_sem.at[3]),
        pltpu.make_async_copy(grad_ref, grad_in, load_sem.at[4]),
    ]
    for load in fetches + loads:
        load.start()

    barrier = pltpu.get_barrier_semaphore()
    peers = (
        [at_x(step(x, k, nx)) for k in range(1, nx)]
        + [at_z(step(z, k, n)) for k in range(1, n)]
        + [at_y(step(y, k, n)) for k in range(1, n)]
        + [pair]
    )
    for peer in peers:
        pl.semaphore_signal(barrier, inc=1, device_id=peer, device_id_type=MESH)

    blank = jnp.zeros((PAD - rows, width), BF16)
    for load in fetches:
        load.wait()
    tok1[x] = jnp.concatenate([tok_in[...], blank], axis=0)
    grad1[z] = jnp.concatenate([grad_in[...], blank], axis=0)

    def keep_matrix(blocks):
        shape = (rows * blocks, PAD * blocks)
        i = lax.broadcasted_iota(jnp.int32, shape, 0)
        j = lax.broadcasted_iota(jnp.int32, shape, 1)
        low = j & (PAD - 1)
        return ((low < rows) & (i == (j >> 3) * rows + low)).astype(F32).astype(BF16)

    pl.semaphore_wait(barrier, len(peers))

    sends = []
    for k in near_first(nx)[::-1]:
        copy = send(tok1.at[x], tok1.at[x], s_tok1.at[k], r_tok1.at[x], at_x(step(x, k, nx)))
        copy.start()
        sends.append(copy)
    for k in near_first(n)[::-1]:
        copy = send(grad1.at[z], grad1.at[z], s_grad1.at[k], r_grad1.at[z], at_z(step(z, k, n)))
        copy.start()
        sends.append(copy)

    def arrived(dst, sem, slot):
        send(dst.at[slot], dst.at[slot], sem.at[slot], sem.at[slot], pair).wait_recv()

    for k in range(1, nx):
        arrived(tok1, r_tok1, step(x, k, nx))
    tok_full[z] = plain(keep_matrix(nx), tok1[...].reshape(nx * PAD, width)).astype(BF16)
    for k in near_first(n):
        copy = send(tok_full.at[z], tok_full.at[z], s_tok2.at[k], r_tok2.at[z], at_z(step(z, k, n)))
        copy.start()
        sends.append(copy)
    for k in range(1, n):
        arrived(grad1, r_grad1, step(z, k, n))
    grad_x[x] = plain(keep_matrix(n), grad1[...].reshape(n * PAD, width)).astype(BF16)
    for k in near_first(nx):
        copy = send(grad_x.at[x], grad_x.at[x], s_grad2.at[k], r_grad2.at[x], at_x(step(x, k, nx)))
        copy.start()
        sends.append(copy)

    for load in loads:
        load.wait()

    def token_group(g):
        @pl.when(g != z)
        def _():
            arrived(tok_full, r_tok2, g)

        return across(tok_full[g], w_all[pl.ds(0, two), :])

    y_copies = []
    for m in range(half):
        g = kept(m, 1 - core)
        pair_src[m] = token_group(g)
        copy = send(pair_src.at[m], pair_dst.at[m], s_pair.at[m], r_pair.at[m], pair)
        copy.start()
        sends.append(copy)
        g = kept(m, core)
        part = token_group(g)
        copy.wait_recv()
        total = part + pair_dst[m]
        y_src[m] = total.astype(BF16)
        copy = send(y_src.at[m], y_dst.at[y], s_y.at[m], r_y.at[y], at_y(g))
        y_copies.append((g, copy))

        @pl.when(g != y)
        def _(copy=copy):
            copy.start()

        @pl.when(g == y)
        def _(total=total):
            own_sum[...] = total

    for k in range(1, nx):
        arrived(grad_x, r_grad2, step(x, k, nx))
    shape = (group * n, group * n)
    i = lax.broadcasted_iota(jnp.int32, shape, 0)
    j = lax.broadcasted_iota(jnp.int32, shape, 1)

    def split(v):
        block = lax.div(v, rows)
        return block >> (nx.bit_length() - 1), block & (nx - 1), v - block * rows

    zi, xi, ti = split(i)
    xj = lax.div(j, rows * n)
    zj = lax.div(j - xj * (rows * n), rows)
    tj = j - (xj * n + zj) * rows
    order = ((zi == zj) & (xi == xj) & (ti == tj)).astype(F32).astype(BF16)
    grad_full[...] = plain(order, grad_x[...].reshape(group * n, width)).astype(BF16)
    back[...] = across(grad_full[...], w_all[pl.ds(two, hidden), :]).reshape(n, group, hidden)

    b_copies = []
    for m in range(half):
        g = kept(m, 1 - core)
        copy = send(back.at[g], back_dst.at[m], s_pairb.at[m], r_pairb.at[m], pair)
        copy.start()
        b_copies.append(copy)
        sends.append(copy)
    yb_copies = []
    for m in range(half):
        g = kept(m, core)
        b_copies[m].wait_recv()
        total = back[g] + back_dst[m]
        yb_src[m] = total.astype(BF16)
        copy = send(yb_src.at[m], yb_dst.at[y], s_yb.at[m], r_yb.at[y], at_y(g))
        yb_copies.append((g, copy))

        @pl.when(g != y)
        def _(copy=copy):
            copy.start()

        @pl.when(g == y)
        def _(total=total):
            own_back[...] = total

    @pl.when(mine(y))
    def _():
        both = own_sum[...]
        for k in range(1, n):
            g = step(y, k, n)
            arrived(y_dst, r_y, g)
            both = both + y_dst[g].astype(F32)
        gate_sum, up_sum = both[:, :hidden], both[:, hidden:]
        back_sum = own_back[...]
        for k in range(1, n):
            g = step(y, k, n)
            arrived(yb_dst, r_yb, g)
            back_sum = back_sum + yb_dst[g].astype(F32)
        sigmoid_gate = 1.0 / (1.0 + jnp.exp(-gate_sum))
        activated = gate_sum * sigmoid_gate
        slope = sigmoid_gate * (1.0 + gate_sum * (1.0 - sigmoid_gate))
        grads = jnp.concatenate([back_sum * up_sum * slope, back_sum * activated], axis=1)
        hid[y, :, pl.ds(0, two)] = grads.astype(BF16)
        hid[y, :, pl.ds(two, hidden)] = (activated * up_sum).astype(BF16)
        for k in near_first(n):
            send(hid.at[y], hid.at[y], s_hid.at[k], r_hid.at[y], at_y(step(y, k, n))).start()

    d_copies = []
    for k in [0] + near_first(n):
        g = step(y, k, n)
        to_pair = send(hid.at[g], hid.at[g], s_fwd.at[k], r_hid.at[g], pair)
        if k == 0:

            @pl.when(jnp.logical_not(mine(g)))
            def _(g=g):
                arrived(hid, r_hid, g)
        else:
            arrived(hid, r_hid, g)

        @pl.when(mine(g))
        def _(to_pair=to_pair):
            to_pair.start()

        part = plain(hid[g, :, pl.ds(0, two)], w_all[pl.ds(0, two), :]).astype(BF16)
        copy = send(d_src.at[g], d_dst.at[z], s_d.at[k], r_d.at[z], at_z(g))
        d_copies.append((g, copy))

        @pl.when(g != z)
        def _(copy=copy, part=part, g=g):
            d_src[g] = part
            copy.start()

        @pl.when(g == z)
        def _(part=part):
            d_dst[z] = part

    tok_all = tok_full[...].reshape(n * group, width)
    grads_all = hid[:, :, pl.ds(0, two)].reshape(n * group, two)
    gg_out[...] = down(grads_all[:, :hidden], tok_all).astype(BF16)
    gu_out[...] = down(grads_all[:, hidden:], tok_all).astype(BF16)

    for k in range(1, n):
        arrived(d_dst, r_d, step(z, k, n))
    spread = keep_matrix(nx)
    spread = jnp.concatenate([spread] * n, axis=0)
    summed = down(spread, d_dst[...].reshape(n * group, width))
    e_src[...] = summed.reshape(nx, PAD, width)
    e_copies = []
    for k in near_first(nx)[::-1]:
        to = step(x, k, nx)
        copy = send(e_src.at[to], e_dst.at[x], s_e.at[k], r_e.at[x], at_x(to))
        copy.start()
        sends.append(copy)

    hidden_all = hid[:, :, pl.ds(two, hidden)].reshape(n * group, hidden)
    gd_out[...] = down(hidden_all, grad_full[...]).astype(BF16)

    total = e_src[x]
    for k in range(1, nx):
        g = step(x, k, nx)
        arrived(e_dst, r_e, g)
        total = total + e_dst[g]
    gtok_ref[...] = total[:rows].astype(BF16)

    for copy in sends:
        copy.wait_send()
    for target, copies in ((y, y_copies), (y, yb_copies), (z, d_copies)):
        for g, copy in copies:

            @pl.when(g != target)
            def _(copy=copy):
                copy.wait_send()

    @pl.when(mine(y))
    def _():
        for k in near_first(n):
            send(hid.at[y], hid.at[y], s_hid.at[k], r_hid.at[y], at_y(step(y, k, n))).wait_send()

    for k in range(n):
        g = step(y, k, n)

        @pl.when(mine(g))
        def _(g=g, k=k):
            send(hid.at[g], hid.at[g], s_fwd.at[k], r_hid.at[g], pair).wait_send()


def shards(n, nx, tokens, grad_out, gate_weight, up_weight, down_weight):
    rows, width = tokens.shape
    hidden = down_weight.shape[0]
    two, group, half = 2 * hidden, rows * nx, n // 2
    dma = pltpu.SemaphoreType.DMA
    out = jax.ShapeDtypeStruct((hidden, width), BF16)
    vmem = pl.BlockSpec(memory_space=pltpu.VMEM)
    hbm = pl.BlockSpec(memory_space=pl.ANY)
    grad_tokens, gate_t, up_t, grad_down = pl.pallas_call(
        functools.partial(kernel, n, nx),
        out_shape=(jax.ShapeDtypeStruct((rows, width), BF16), out, out, out),
        in_specs=[hbm] * 5,
        out_specs=(vmem,) * 4,
        scratch_shapes=[
            pltpu.VMEM((rows, width), BF16),
            pltpu.VMEM((rows, width), BF16),
            pltpu.VMEM((3 * hidden, width), BF16),
            pltpu.VMEM((nx, PAD, width), BF16),
            pltpu.VMEM((n, PAD, width), BF16),
            pltpu.VMEM((n, group, width), BF16),
            pltpu.VMEM((nx, group, width), BF16),
            pltpu.VMEM((n * group, width), BF16),
            pltpu.VMEM((half, group, two), F32),
            pltpu.VMEM((half, group, two), F32),
            pltpu.VMEM((group, two), F32),
            pltpu.VMEM((half, group, two), BF16),
            pltpu.VMEM((n, group, two), BF16),
            pltpu.VMEM((n, group, hidden), F32),
            pltpu.VMEM((half, group, hidden), F32),
            pltpu.VMEM((group, hidden), F32),
            pltpu.VMEM((half, group, hidden), BF16),
            pltpu.VMEM((n, group, hidden), BF16),
            pltpu.VMEM((n, group, 3 * hidden), BF16),
            pltpu.VMEM((n, group, width), BF16),
            pltpu.VMEM((n, group, width), BF16),
            pltpu.VMEM((nx, PAD, width), F32),
            pltpu.VMEM((nx, PAD, width), F32),
            dma((5,)),
            dma((nx,)), dma((nx,)), dma((n,)), dma((n,)), dma((n,)), dma((n,)), dma((nx,)), dma((nx,)),
            dma((half,)), dma((half,)), dma((half,)), dma((n,)), dma((half,)), dma((half,)), dma((half,)), dma((n,)),
            dma((n,)), dma((n,)), dma((n,)), dma((n,)), dma((n,)), dma((nx,)), dma((nx,)),
        ],
        compiler_params=pltpu.CompilerParams(
            collective_id=0, has_side_effects=True, vmem_limit_bytes=67043328
        ),
        name="block",
    )(tokens, grad_out, gate_weight.T, up_weight.T, down_weight)
    return grad_tokens, gate_t.T, up_t.T, grad_down


def solution(mesh):
    n = mesh.shape["row"] // 2
    nx = mesh.shape["col"] // n
    placed = (P("col", "row"), P("col", "row"), P("row", "col"), P("row", "col"), P("col", "row"))
    return jax.shard_map(
        functools.partial(shards, n, nx),
        mesh=mesh,
        in_specs=placed,
        out_specs=(P("col", "row"), P("row", "col"), P("row", "col"), P("col", "row")),
        check_vma=False,
    )
```

time: 190 us -> 83.3 us (0.44)
  the two profiles are of different devices: /device:TPU:6 before, /device:TPU:48 now
where the time goes in v1:
time: 83.3 us; the launch traced here: 83 us
  Pallas kernels  77.2 us (93%)
  local copies, waits for them, and re-layouts  5.11 us (6%)
    pallas_call x1, Pallas kernels, shards(): pl.pallas_call(functools.partial(kernel, n, nx), out_shape=(jax.ShapeDtyp...  77.2 us
    unnamed x10, local copies, waits for them, and re-layouts  5.11 us

profile of v1, /device:TPU:48, one launch (start us, length us, event | category | flops | bytes accessed | tf_op | source)
XLA Modules:
  0.0 83.0 jit_solution(4809764380466718425)
XLA Ops:
  0.6 77.2 %block.1 = (bf16[5,512]{1,0:T(8,128)(2,1)}, bf16[448,512]{1,0:T(8,128)(2,1)}, bf16[448,512]{1,0:T(8,128)(2,1)}, bf16[448,512]{1,0:T(8,128)(2,1)}) custom-call(bf16[5,512]{1,0:T(8,128)(2,1)} %tok_ref.1, bf16[5,512]{1,0:T(8,128)(2,1)} %grad_ref.1, bf16[448,512]{1,0:T(8,128)(2,1)} %bitcast.6, bf16[448,512]{1,0:T(8,128)(2,1)} %bitcast.7, bf16[448,512]{1,0:T(8,128)(2,1)} %wd_ref.1), custom_call_target="tpu_custom_call" | custom-call | tf_op jit(solution)/shard_map/block/pallas_call | solution.py:335
  77.9 0.0 copy-start.2
  77.9 0.7 copy-done.2
  78.6 0.6 copy.13
  79.2 0.0 copy-start.1
  79.2 1.9 %copy.14 = bf16[512,448]{0,1:T(8,128)(2,1)} copy(bf16[512,448]{0,1:T(8,128)(2,1)} %bitcast.5) | data formatting | bytes 917504
  81.0 0.0 copy-done.1
  81.0 0.0 copy-start
  81.0 0.8 copy.15
  81.8 0.4 copy-done
  82.2 0.8 copy.16
Async XLA Ops:
  77.9 0.7 copy-start.2
  79.2 1.9 %copy-start.1 = (bf16[448,512]{1,0:T(8,128)(2,1)S(1)}, bf16[448,512]{1,0:T(8,128)(2,1)}, u32[]{:S(2)}) copy-start(bf16[448,512]{1,0:T(8,128)(2,1)} %get-tuple-element.10) | copy-start | bytes 1376260
  81.0 1.2 %copy-start = (bf16[448,512]{1,0:T(8,128)(2,1)S(1)}, bf16[448,512]{1,0:T(8,128)(2,1)}, u32[]{:S(2)}) copy-start(bf16[448,512]{1,0:T(8,128)(2,1)} %get-tuple-element.19) | copy-start | bytes 1376260

commit v2 on v0

v2 whole, which is shorter than its diff:
```python
import functools

import jax
import jax.numpy as jnp
from jax import lax
from jax.experimental import pallas as pl
from jax.experimental.pallas import tpu as pltpu
from jax.sharding import PartitionSpec as P

MESH = pl.DeviceIdType.MESH
BF16 = jnp.bfloat16
F32 = jnp.float32
PAD = 8
LANES = 128
MIB = 1024 * 1024


def near_first(n):
    order = []
    for k in range(1, n // 2 + 1):
        order.append(k)
        if n - k != k:
            order.append(n - k)
    return order


def spaced(n, odd):
    return [0] * (1 - odd) + [k for k in near_first(n) if k % 2 == odd]


def groups_of(n):
    half = n // 2
    ks = ([(n - m) % n for m in range(half)], [m + 1 for m in range(half)])
    if n == 8:
        owners = ([0, 4, 1, 5], [2, 6, 3, 7])
    else:
        owners = (list(range(half)), list(range(half, n)))
    return ks, owners


def across(a, b):
    return lax.dot_general(a, b, (((1,), (1,)), ((), ())), preferred_element_type=F32)


def down(a, b):
    return lax.dot_general(a, b, (((0,), (0,)), ((), ())), preferred_element_type=F32)


def plain(a, b):
    return lax.dot_general(a, b, (((1,), (0,)), ((), ())), preferred_element_type=F32)


def iota(shape, dim):
    return lax.broadcasted_iota(jnp.int32, shape, dim)


def ones_where(mask):
    return mask.astype(F32).astype(BF16)


def kernel(
    n,
    tok_ref, grad_ref, wg_ref, wu_ref, wd_ref,
    gtok_ref, gg_out, gu_out, gd_out,
    tok_in, grad_in, packed, w_all, blocks, tok_full, grad_full,
    pair_src, pair_dst, own_sum, y_src, y_dst, hid_g, hid_h, d_src, d_dst, e_src, e_dst,
    load_sem, s_own, s_blk, r_blk, s_pair, r_pair, s_y, r_y, s_hid, r_hid, s_fwd, s_hidh, r_hidh, s_fwdh, s_d, r_d, s_e, r_e,
):
    rows, width = tok_in.shape
    hidden = wd_ref.shape[0]
    two = 2 * hidden
    half = n // 2
    side = rows * half
    group = 2 * side
    room = d_src.shape[2]
    parts = 2 * width // LANES
    block = rows * parts

    row, col = lax.axis_index("row"), lax.axis_index("col")
    y, core = lax.div(row, 2), lax.rem(row, 2)
    z, x = lax.div(col, n), lax.rem(col, n)
    odd = lax.rem(z + x, 2)
    pair = (row + 1 - 2 * core, col)
    spot = x + odd * (z - x)
    here = lax.div(spot, 2)

    def step(a, k):
        return lax.rem(a + k, n)

    def at_x(k):
        return (row, z * n + k)

    def at_z(k):
        return (row, k * n + x)

    def at_y(k):
        return (2 * k + core, col)

    def at_own(k):
        other = step(spot, k)
        return (row, (z * n + other) * (1 - odd) + (other * n + x) * odd)

    def send(src, dst, s, r, device):
        return pltpu.make_async_remote_copy(
            src_ref=src, dst_ref=dst, send_sem=s, recv_sem=r, device_id=device, device_id_type=MESH
        )

    def arrived(dst, sem):
        send(dst, dst, sem, sem, pair).wait_recv()

    ks, owners = groups_of(n)

    def pick(first, second, who):
        return first * (1 - who) + second * who

    def kept(m, who):
        return pick(ks[0][m], ks[1][m], who), pick(owners[0][m], owners[1][m], who)

    def mine(o):
        found = [o == pick(owners[0][m], owners[1][m], core) for m in range(half)]
        return functools.reduce(jnp.logical_or, found)

    def distance(o):
        return sum(jnp.where(o == owners[w][m], ks[w][m], 0) for w in range(2) for m in range(half))

    sends = []
    y_copies, d_copies, e_copies = [], [], []

    def drain():
        for copy in sends:
            copy.wait_send()
        for clash, copy in y_copies + d_copies + e_copies:

            @pl.when(jnp.logical_not(clash))
            def _(copy=copy):
                copy.wait_send()

    fetches = [
        pltpu.make_async_copy(tok_ref, tok_in, load_sem.at[0]),
        pltpu.make_async_copy(grad_ref, grad_in, load_sem.at[1]),
    ]
    loads = [
        pltpu.make_async_copy(wg_ref, w_all.at[pl.ds(0, hidden)], load_sem.at[2]),
        pltpu.make_async_copy(wu_ref, w_all.at[pl.ds(hidden, hidden)], load_sem.at[3]),
        pltpu.make_async_copy(wd_ref, w_all.at[pl.ds(two, hidden)], load_sem.at[4]),
    ]
    for load in fetches + loads:
        load.start()

    barrier = pltpu.get_barrier_semaphore()
    peers = [at(step(a, k)) for at, a in ((at_x, x), (at_z, z), (at_y, y)) for k in range(1, n)] + [pair]
    for peer in peers:
        pl.semaphore_signal(barrier, inc=1, device_id=peer, device_id_type=MESH)

    for load in fetches:
        load.wait()
    for a, ref in enumerate((tok_in, grad_in)):
        value = ref[...].astype(F32)
        for q in range(parts // 2):
            at = (a * (parts // 2) + q) * rows
            packed[pl.ds(at, rows), :] = value[:, q * LANES : (q + 1) * LANES]
    blocks[odd, 0, here] = packed[...].astype(BF16)

    total_rows = n * block
    v = iota((1, total_rows), 1)
    b = lax.div(v, block)
    q = lax.div(v - b * block, rows)
    to = q * (n * rows) + b * rows + (v - b * block - q * rows)
    regroup = ones_where(iota((total_rows, total_rows), 0) == to)

    pl.semaphore_wait(barrier, len(peers))

    own = blocks.at[odd, 0, here]
    for k in near_first(n)[::-1]:
        copy = send(own, own, s_own.at[k], r_blk.at[odd, 0, here], at_own(k))
        copy.start()
        sends.append(copy)
    same, differ = spaced(n, 0), spaced(n, 1)
    for s in range(half):
        for axis in range(2):
            is_own = odd == axis
            offset = jnp.where(is_own, same[s], differ[s])
            place = lax.div(step(z if axis else x, offset), 2)
            if s == 0:

                @pl.when(jnp.logical_not(is_own))
                def _(axis=axis, place=place):
                    arrived(blocks.at[axis, 0, place], r_blk.at[axis, 0, place])
            else:
                arrived(blocks.at[axis, 0, place], r_blk.at[axis, 0, place])
            for k in near_first(n):
                device = at_x(step(x, k)) if axis else at_z(step(z, k))
                copy = send(
                    blocks.at[axis, 0, place], blocks.at[axis, k, place],
                    s_blk.at[axis, k, s], r_blk.at[axis, k, place], device,
                )
                copy.start()
                sends.append(copy)

    for load in loads:
        load.wait()

    def partial(pairs):
        for k, _ in pairs:

            @pl.when(k != 0)
            def _(k=k):
                for axis in range(2):
                    for i in range(half):
                        arrived(blocks.at[axis, k, i], r_blk.at[axis, k, i])

        held = [
            jnp.concatenate([blocks[axis, k].reshape(half * block, LANES) for axis in range(2)], axis=0)
            for k, _ in pairs
        ]
        rows_of = plain(regroup, jnp.concatenate(held, axis=1)).astype(BF16)
        toks, grads = [], []
        for at, (_, o) in enumerate(pairs):
            lanes = rows_of[:, at * LANES : (at + 1) * LANES]
            cut = [lanes[q * group : (q + 1) * group] for q in range(parts)]
            toks.append(jnp.concatenate(cut[: parts // 2], axis=1))
            grads.append(jnp.concatenate(cut[parts // 2 :], axis=1))
            tok_full[o] = toks[-1]
            grad_full[o] = grads[-1]
        sums = across(jnp.concatenate(toks, axis=0), w_all[pl.ds(0, two), :])
        backs = across(jnp.concatenate(grads, axis=0), w_all[pl.ds(two, hidden), :])
        return jnp.concatenate([sums, backs], axis=1)

    batch = max(half // 2, 1)
    for m in range(0, half, batch):
        spots = range(m, m + batch)
        pair_src[m // batch] = partial([kept(i, 1 - core) for i in spots])
        copy = send(pair_src.at[m // batch], pair_dst.at[m // batch], s_pair.at[m], r_pair.at[m], pair)
        copy.start()
        sends.append(copy)
        part = partial([kept(i, core) for i in spots])
        copy.wait_recv()
        sums = part + pair_dst[m // batch]
        for at, i in enumerate(spots):
            _, g = kept(i, core)
            total = sums[at * group : (at + 1) * group]
            y_src[i] = total.astype(BF16)
            copy = send(y_src.at[i], y_dst.at[y], s_y.at[i], r_y.at[y], at_y(g))
            y_copies.append((g == y, copy))

            @pl.when(g != y)
            def _(copy=copy):
                copy.start()

            @pl.when(g == y)
            def _(total=total):
                own_sum[...] = total

    hid_order = near_first(n)
    direct = hid_order

    def handed_drain(lists):
        for ref, s_out, s_pass, r in lists:

            @pl.when(mine(y))
            def _(ref=ref, s_out=s_out, r=r):
                for copy in from_owner(ref, s_out, r):
                    copy.wait_send()

            for k in range(n):
                copy = to_pair(ref, s_pass, r, k)
                pl.when(mine(step(y, k)))(copy.wait_send)

    def from_owner(ref, s, r):
        return [send(ref.at[y], ref.at[y], s.at[k], r.at[y], at_y(step(y, k))) for k in direct]

    def to_pair(ref, s, r, k):
        g = step(y, k)
        return send(ref.at[g], ref.at[g], s.at[k], r.at[g], pair)

    def hand_on(ref, s, r, k):
        g = step(y, k)
        if k == 0:
            pl.when(jnp.logical_not(mine(g)))(lambda: arrived(ref.at[g], r.at[g]))
        else:
            arrived(ref.at[g], r.at[g])
        pl.when(mine(g))(lambda: to_pair(ref, s, r, k).start())

    @pl.when(mine(y))
    def _():
        all_sums = own_sum[...]
        for k in hid_order:
            g = step(y, k)
            arrived(y_dst.at[g], r_y.at[g])
            all_sums = all_sums + y_dst[g].astype(F32)
        gate_sum, up_sum, back_sum = all_sums[:, :hidden], all_sums[:, hidden:two], all_sums[:, two:]
        sigmoid_gate = 1.0 / (1.0 + jnp.exp(-gate_sum))
        activated = gate_sum * sigmoid_gate
        slope = sigmoid_gate * (1.0 + gate_sum * (1.0 - sigmoid_gate))
        grads = jnp.concatenate([back_sum * up_sum * slope, back_sum * activated], axis=1)
        hid_g[y] = grads.astype(BF16)
        for copy in from_owner(hid_g, s_hid, r_hid):
            copy.start()
        hid_h[y] = (activated * up_sum).astype(BF16)
        for copy in from_owner(hid_h, s_hidh, r_hidh):
            copy.start()

    def apart_for(count):
        i, j = iota((2 * room * count, 1), 0), iota((1, group * count), 1)
        block_of = lax.div(j, side)
        return ones_where(i == block_of * room + j - block_of * side)

    offsets = [0] + hid_order
    middle = n // 2 + 1
    for near in (offsets[:middle], offsets[middle:]):
        for k in near:
            hand_on(hid_g, s_fwd, r_hid, k)
        if not near:
            continue
        grads = jnp.concatenate([hid_g[step(y, k)] for k in near], axis=0)
        part = plain(grads, w_all[pl.ds(0, two), :]).astype(BF16)
        part = plain(apart_for(len(near)), part).astype(BF16)
        for at, k in enumerate(near):
            g = distance(step(y, k))
            home = g == 0
            for axis, a, place in ((0, z, at_z), (1, x, at_x)):
                device = place(step(a, n - g))
                first = (2 * at + axis) * room
                piece = part[first : first + room]
                d_src[axis, g] = piece
                copy = send(d_src.at[axis, g], d_dst.at[axis, g], s_d.at[axis, g], r_d.at[axis, g], device)
                d_copies.append((home, copy))

                @pl.when(jnp.logical_not(home))
                def _(copy=copy):
                    copy.start()

                @pl.when(home)
                def _(axis=axis, piece=piece):
                    d_dst[axis, 0] = piece

    for k in offsets:
        hand_on(hid_h, s_fwdh, r_hidh, k)

    tok_all = tok_full[...].reshape(n * group, width)
    grads_all = hid_g[...].reshape(n * group, two)
    gg_out[...] = down(grads_all[:, :hidden], tok_all).astype(BF16)
    gu_out[...] = down(grads_all[:, hidden:], tok_all).astype(BF16)

    i, j = iota((half * PAD, room), 0), iota((half * PAD, room), 1)
    low = i & (PAD - 1)
    spread = ones_where((low < rows) & (j == (i >> 3) * rows + low))
    spread = jnp.concatenate([spread] * n, axis=1)
    for axis in range(2):
        for k in range(1, n):
            arrived(d_dst.at[axis, k], r_d.at[axis, k])
        summed = plain(spread, d_dst[axis].reshape(n * room, width))
        e_src[axis] = summed.reshape(half, PAD, width)
        line, cross = (z, x) if axis else (x, z)
        for i in range(half):
            place = 2 * i + lax.rem(cross + axis, 2)
            device = at_z(place) if axis else at_x(place)
            is_self = place == line
            copy = send(e_src.at[axis, i], e_dst.at[line], s_e.at[axis, i], r_e.at[line], device)
            e_copies.append((is_self, copy))

            @pl.when(jnp.logical_not(is_self))
            def _(copy=copy):
                copy.start()

            @pl.when(is_self)
            def _(axis=axis, i=i, line=line):
                e_dst[line] = e_src[axis, i]

    grad_all = grad_full[...].reshape(n * group, width)
    hidden_all = hid_h[...].reshape(n * group, hidden)
    gd_out[...] = down(hidden_all, grad_all).astype(BF16)

    for k in range(1, n):
        g = step(spot, k)
        arrived(e_dst.at[g], r_e.at[g])
    gtok_ref[...] = jnp.sum(e_dst[...], axis=0)[:rows].astype(BF16)

    drain()
    handed_drain(((hid_g, s_hid, s_fwd, r_hid), (hid_h, s_hidh, s_fwdh, r_hidh)))


def put_out(*refs):
    count = (len(refs) - 1) // 2
    copies = [pltpu.make_async_copy(refs[i], refs[count + i], refs[-1].at[i]) for i in range(count)]
    for copy in copies:
        copy.start()
    for copy in copies:
        copy.wait()


def shards(n, tokens, grad_out, gate_weight, up_weight, down_weight):
    rows, width = tokens.shape
    hidden = down_weight.shape[0]
    two, half = 2 * hidden, n // 2
    side = rows * half
    batch = max(half // 2, 1)
    group = 2 * side
    room = -(-side // PAD) * PAD
    block = rows * 2 * width // LANES
    dma = pltpu.SemaphoreType.DMA
    out = jax.ShapeDtypeStruct((hidden, width), BF16)
    outs = (jax.ShapeDtypeStruct((rows, width), BF16), out, out, out)
    vmem = pl.BlockSpec(memory_space=pltpu.VMEM)
    hbm = pl.BlockSpec(memory_space=pltpu.HBM)
    results = pl.pallas_call(
        functools.partial(kernel, n),
        out_shape=outs,
        in_specs=[hbm] * 5,
        out_specs=(vmem,) * 4,
        scratch_shapes=[
            pltpu.VMEM((rows, width), BF16),
            pltpu.VMEM((rows, width), BF16),
            pltpu.VMEM((block, LANES), F32),
            pltpu.VMEM((3 * hidden, width), BF16),
            pltpu.VMEM((2, n, half, block, LANES), BF16),
            pltpu.VMEM((n, group, width), BF16),
            pltpu.VMEM((n, group, width), BF16),
            pltpu.VMEM((half // batch, batch * group, 3 * hidden), F32),
            pltpu.VMEM((half // batch, batch * group, 3 * hidden), F32),
            pltpu.VMEM((group, 3 * hidden), F32),
            pltpu.VMEM((half, group, 3 * hidden), BF16),
            pltpu.VMEM((n, group, 3 * hidden), BF16),
            pltpu.VMEM((n, group, two), BF16),
            pltpu.VMEM((n, group, hidden), BF16),
            pltpu.VMEM((2, n, room, width), BF16),
            pltpu.VMEM((2, n, room, width), BF16),
            pltpu.VMEM((2, half, PAD, width), F32),
            pltpu.VMEM((n, PAD, width), F32),
            dma((5,)),
            dma((n,)), dma((2, n, half)), dma((2, n, half)),
            dma((half,)), dma((half,)), dma((half,)), dma((n,)),
            dma((n,)), dma((n,)), dma((n,)), dma((n,)), dma((n,)), dma((n,)),
            dma((2, n)), dma((2, n)), dma((2, half)), dma((n,)),
        ],
        compiler_params=pltpu.CompilerParams(collective_id=0, has_side_effects=True, vmem_limit_bytes=32 * MIB),
        name="block",
    )(*[pltpu.with_memory_space_constraint(v, pltpu.HBM) for v in (tokens, grad_out, gate_weight.T, up_weight.T, down_weight)])
    grad_tokens, gate_t, up_t, grad_down = pl.pallas_call(
        put_out,
        out_shape=outs,
        in_specs=[vmem] * 4,
        out_specs=(hbm,) * 4,
        scratch_shapes=[dma((4,))],
        compiler_params=pltpu.CompilerParams(vmem_limit_bytes=16 * MIB),
        name="put_out",
    )(*results)
    return grad_tokens, gate_t.T, up_t.T, grad_down


def solution(mesh):
    n = mesh.shape["row"] // 2
    placed = (P("col", "row"), P("col", "row"), P("row", "col"), P("row", "col"), P("col", "row"))
    return jax.shard_map(
        functools.partial(shards, n),
        mesh=mesh,
        in_specs=placed,
        out_specs=(P("col", "row"), P("row", "col"), P("row", "col"), P("col", "row")),
        check_vma=False,
    )
```

time: 190 us -> 77.3 us (0.41)
  the two profiles are of different devices: /device:TPU:6 before, /device:TPU:17 now
where the time goes in v2:
time: 77.3 us; the launch traced here: 77.2 us
  Pallas kernels  76.5 us (99%)
    pallas_call x1, Pallas kernels, shards(): pl.pallas_call(functools.partial(kernel, n), out_shape=outs, in_specs=[hb...  75.4 us

profile of v2, /device:TPU:17, one launch (start us, length us, event | category | flops | bytes accessed | tf_op | source)
XLA Modules:
  0.0 77.2 jit_solution(10595574018618815931)
XLA Ops:
  0.6 75.4 %block.1 = (bf16[5,512]{1,0:T(8,128)(2,1)S(1)}, bf16[448,512]{1,0:T(8,128)(2,1)S(1)}, bf16[448,512]{1,0:T(8,128)(2,1)S(1)}, bf16[448,512]{1,0:T(8,128)(2,1)S(1)}) custom-call(bf16[5,512]{1,0:T(8,128)(2,1)} %tok_ref.1, bf16[5,512]{1,0:T(8,128)(2,1)} %grad_ref.1, bf16[448,512]{1,0:T(8,128)(2,1)} %bitcast.4, bf16[448,512]{1,0:T(8,128)(2,1)} %bitcast.5, ...), custom_call_target="tpu_custom_call" | custom-call | tf_op jit(solution)/shard_map/block/pallas_call | solution.py:406
  76.0 1.1 %put_out.1 = (bf16[5,512]{1,0:T(8,128)(2,1)}, bf16[448,512]{1,0:T(8,128)(2,1)}, bf16[448,512]{1,0:T(8,128)(2,1)}, bf16[448,512]{1,0:T(8,128)(2,1)}) custom-call(bf16[5,512]{1,0:T(8,128)(2,1)S(1)} %get-tuple-element.12.refs_0_, bf16[448,512]{1,0:T(8,128)(2,1)S(1)} %get-tuple-element.13.refs_1_, bf16[448,512]{1,0:T(8,128)(2,1)S(1)} %get-tuple-element.14.refs_2_, ...), custom_call_target="tpu_custom_call" | custom-call | tf_op jit(solution)/shard_map/put_out/pallas_call | solution.py:439

commit v3 on v2

--- a/solution.py
+++ b/solution.py
@@ -38,10 +38,6 @@
     return ks, owners
 
 
-def across(a, b):
-    return lax.dot_general(a, b, (((1,), (1,)), ((), ())), preferred_element_type=F32)
-
-
 def down(a, b):
     return lax.dot_general(a, b, (((0,), (0,)), ((), ())), preferred_element_type=F32)
 
@@ -62,7 +58,7 @@
     n,
     tok_ref, grad_ref, wg_ref, wu_ref, wd_ref,
     gtok_ref, gg_out, gu_out, gd_out,
-    tok_in, grad_in, packed, w_all, blocks, tok_full, grad_full,
+    tok_in, grad_in, packed, w_all, w_turned, blocks, tok_full, grad_full,
     pair_src, pair_dst, own_sum, y_src, y_dst, hid_g, hid_h, d_src, d_dst, e_src, e_dst,
     load_sem, s_own, s_blk, r_blk, s_pair, r_pair, s_y, r_y, s_hid, r_hid, s_fwd, s_hidh, r_hidh, s_fwdh, s_d, r_d, s_e, r_e,
 ):
@@ -100,6 +96,9 @@
         other = step(spot, k)
         return (row, (z * n + other) * (1 - odd) + (other * n + x) * odd)
 
+    def at_cross(k):
+        return (row, (z * n + step(x, k)) * odd + (step(z, k) * n + x) * (1 - odd))
+
     def send(src, dst, s, r, device):
         return pltpu.make_async_remote_copy(
             src_ref=src, dst_ref=dst, send_sem=s, recv_sem=r, device_id=device, device_id_type=MESH
@@ -175,30 +174,35 @@
         copy = send(own, own, s_own.at[k], r_blk.at[odd, 0, here], at_own(k))
         copy.start()
         sends.append(copy)
-    same, differ = spaced(n, 0), spaced(n, 1)
-    for s in range(half):
-        for axis in range(2):
-            is_own = odd == axis
-            offset = jnp.where(is_own, same[s], differ[s])
-            place = lax.div(step(z if axis else x, offset), 2)
-            if s == 0:
-
-                @pl.when(jnp.logical_not(is_own))
-                def _(axis=axis, place=place):
-                    arrived(blocks.at[axis, 0, place], r_blk.at[axis, 0, place])
-            else:
-                arrived(blocks.at[axis, 0, place], r_blk.at[axis, 0, place])
-            for k in near_first(n):
-                device = at_x(step(x, k)) if axis else at_z(step(z, k))
-                copy = send(
-                    blocks.at[axis, 0, place], blocks.at[axis, k, place],
-                    s_blk.at[axis, k, s], r_blk.at[axis, k, place], device,
-                )
-                copy.start()
-                sends.append(copy)
+    for k in near_first(n):
+        copy = send(own, blocks.at[odd, k, here], s_blk.at[odd, k, 0], r_blk.at[odd, k, here], at_cross(k))
+        copy.start()
+        sends.append(copy)
 
     for load in loads:
         load.wait()
+    for first in range(0, 3 * hidden, LANES):
+        size = min(LANES, 3 * hidden - first)
+        w_turned[:, pl.ds(first, size)] = w_all[pl.ds(first, size), :].T
+
+    same, differ = spaced(n, 0), spaced(n, 1)
+
+    def relay(axis, offset, s):
+        place = lax.div(step(pick(x, z, axis), offset), 2)
+        arrived(blocks.at[axis, 0, place], r_blk.at[axis, 0, place])
+        for k in near_first(n):
+            to_x, to_z = at_x(step(x, k))[1], at_z(step(z, k))[1]
+            copy = send(
+                blocks.at[axis, 0, place], blocks.at[axis, k, place],
+                s_blk.at[axis, k, s], r_blk.at[axis, k, place], (row, pick(to_z, to_x, axis)),
+            )
+            copy.start()
+            sends.append(copy)
+
+    for s in range(half):
+        relay(1 - odd, differ[s], s)
+        if s + 1 < half:
+            relay(odd, same[s + 1], s + 1)
 
     def partial(pairs):
         for k, _ in pairs:
@@ -222,8 +226,8 @@
             grads.append(jnp.concatenate(cut[parts // 2 :], axis=1))
             tok_full[o] = toks[-1]
             grad_full[o] = grads[-1]
-        sums = across(jnp.concatenate(toks, axis=0), w_all[pl.ds(0, two), :])
-        backs = across(jnp.concatenate(grads, axis=0), w_all[pl.ds(two, hidden), :])
+        sums = plain(jnp.concatenate(toks, axis=0), w_turned[:, pl.ds(0, two)])
+        backs = plain(jnp.concatenate(grads, axis=0), w_turned[:, pl.ds(two, hidden)])
         return jnp.concatenate([sums, backs], axis=1)
 
     batch = max(half // 2, 1)
@@ -275,11 +279,16 @@
 
     def hand_on(ref, s, r, k):
         g = step(y, k)
-        if k == 0:
-            pl.when(jnp.logical_not(mine(g)))(lambda: arrived(ref.at[g], r.at[g]))
-        else:
-            arrived(ref.at[g], r.at[g])
-        pl.when(mine(g))(lambda: to_pair(ref, s, r, k).start())
+
+        @pl.when(mine(g))
+        def _():
+            if k:
+                arrived(ref.at[g], r.at[g])
+            to_pair(ref, s, r, k).start()
+
+    def handed(ref, r, k):
+        g = step(y, k)
+        pl.when(jnp.logical_not(mine(g)))(lambda: arrived(ref.at[g], r.at[g]))
 
     @pl.when(mine(y))
     def _():
@@ -297,8 +306,12 @@
         for copy in from_owner(hid_g, s_hid, r_hid):
             copy.start()
         hid_h[y] = (activated * up_sum).astype(BF16)
-        for copy in from_owner(hid_h, s_hidh, r_hidh):
-            copy.start()
+
+    def hidden_out():
+        @pl.when(mine(y))
+        def _():
+            for copy in from_owner(hid_h, s_hidh, r_hidh):
+                copy.start()
 
     def apart_for(count):
         i, j = iota((2 * room * count, 1), 0), iota((1, group * count), 1)
@@ -310,8 +323,13 @@
     for near in (offsets[:middle], offsets[middle:]):
         for k in near:
             hand_on(hid_g, s_fwd, r_hid, k)
+        for k in near:
+            handed(hid_g, r_hid, k)
         if not near:
+            hidden_out()
             continue
+        if near[0]:
+            hidden_out()
         grads = jnp.concatenate([hid_g[step(y, k)] for k in near], axis=0)
         part = plain(grads, w_all[pl.ds(0, two), :]).astype(BF16)
         part = plain(apart_for(len(near)), part).astype(BF16)
@@ -333,9 +351,6 @@
                 @pl.when(home)
                 def _(axis=axis, piece=piece):
                     d_dst[axis, 0] = piece
-
-    for k in offsets:
-        hand_on(hid_h, s_fwdh, r_hidh, k)
 
     tok_all = tok_full[...].reshape(n * group, width)
     grads_all = hid_g[...].reshape(n * group, two)
@@ -366,6 +381,11 @@
             @pl.when(is_self)
             def _(axis=axis, i=i, line=line):
                 e_dst[line] = e_src[axis, i]
+
+    for k in offsets:
+        hand_on(hid_h, s_fwdh, r_hidh, k)
+    for k in offsets:
+        handed(hid_h, r_hidh, k)
 
     grad_all = grad_full[...].reshape(n * group, width)
     hidden_all = hid_h[...].reshape(n * group, hidden)
@@ -413,6 +433,7 @@
             pltpu.VMEM((rows, width), BF16),
             pltpu.VMEM((block, LANES), F32),
             pltpu.VMEM((3 * hidden, width), BF16),
+            pltpu.VMEM((width, 3 * hidden), BF16),
             pltpu.VMEM((2, n, half, block, LANES), BF16),
             pltpu.VMEM((n, group, width), BF16),
             pltpu.VMEM((n, group, width), BF16),

time: 77.3 us -> 73.3 us (0.948)
  the two profiles are of different devices: /device:TPU:17 before, /device:TPU:23 now
where the time goes in v3:
time: 73.3 us; the launch traced here: 73.2 us
  Pallas kernels  72.5 us (99%)
    pallas_call x1, Pallas kernels, shards(): pl.pallas_call(functools.partial(kernel, n), out_shape=outs, in_specs=[hb...  71.4 us

profile of v3, /device:TPU:23, one launch (start us, length us, event | category | flops | bytes accessed | tf_op | source)
XLA Modules:
  0.0 73.2 jit_solution(4051680336777663714)
XLA Ops:
  0.6 71.4 %block.1 = (bf16[5,512]{1,0:T(8,128)(2,1)S(1)}, bf16[448,512]{1,0:T(8,128)(2,1)S(1)}, bf16[448,512]{1,0:T(8,128)(2,1)S(1)}, bf16[448,512]{1,0:T(8,128)(2,1)S(1)}) custom-call(bf16[5,512]{1,0:T(8,128)(2,1)} %tok_ref.1, bf16[5,512]{1,0:T(8,128)(2,1)} %grad_ref.1, bf16[448,512]{1,0:T(8,128)(2,1)} %bitcast.4, bf16[448,512]{1,0:T(8,128)(2,1)} %bitcast.5, ...), custom_call_target="tpu_custom_call" | custom-call | tf_op jit(solution)/shard_map/block/pallas_call | solution.py:426
  72.1 1.1 %put_out.1 = (bf16[5,512]{1,0:T(8,128)(2,1)}, bf16[448,512]{1,0:T(8,128)(2,1)}, bf16[448,512]{1,0:T(8,128)(2,1)}, bf16[448,512]{1,0:T(8,128)(2,1)}) custom-call(bf16[5,512]{1,0:T(8,128)(2,1)S(1)} %get-tuple-element.12.refs_0_, bf16[448,512]{1,0:T(8,128)(2,1)S(1)} %get-tuple-element.13.refs_1_, bf16[448,512]{1,0:T(8,128)(2,1)S(1)} %get-tuple-element.14.refs_2_, ...), custom_call_target="tpu_custom_call" | custom-call | tf_op jit(solution)/shard_map/put_out/pallas_call | solution.py:460

commit v4 on v3

--- a/solution.py
+++ b/solution.py
@@ -199,10 +199,10 @@
             copy.start()
             sends.append(copy)
 
-    for s in range(half):
-        relay(1 - odd, differ[s], s)
-        if s + 1 < half:
-            relay(odd, same[s + 1], s + 1)
+    waits = [(min(k, n - k), 1, s, k) for s, k in enumerate(differ)]
+    waits += [(min(k, n - k), 0, s, k) for s, k in enumerate(same) if s]
+    for _, crossed, s, k in sorted(waits):
+        relay(1 - odd if crossed else odd, k, s)
 
     def partial(pairs):
         for k, _ in pairs:

time: 73.3 us -> 73.4 us (level)
  no operation moved by 1% of the time
where the time goes in v4:
time: 73.4 us; the launch traced here: 72.8 us
  Pallas kernels  72.2 us (98%)
    pallas_call x1, Pallas kernels, shards(): pl.pallas_call(functools.partial(kernel, n), out_shape=outs, in_specs=[hb...  71 us

profile of v4, /device:TPU:23, one launch (start us, length us, event | category | flops | bytes accessed | tf_op | source)
XLA Modules:
  0.0 72.8 jit_solution(5167436881307108113)
XLA Ops:
  0.6 71.0 %block.1 = (bf16[5,512]{1,0:T(8,128)(2,1)S(1)}, bf16[448,512]{1,0:T(8,128)(2,1)S(1)}, bf16[448,512]{1,0:T(8,128)(2,1)S(1)}, bf16[448,512]{1,0:T(8,128)(2,1)S(1)}) custom-call(bf16[5,512]{1,0:T(8,128)(2,1)} %tok_ref.1, bf16[5,512]{1,0:T(8,128)(2,1)} %grad_ref.1, bf16[448,512]{1,0:T(8,128)(2,1)} %bitcast.4, bf16[448,512]{1,0:T(8,128)(2,1)} %bitcast.5, ...), custom_call_target="tpu_custom_call" | custom-call | tf_op jit(solution)/shard_map/block/pallas_call | solution.py:426
  71.7 1.1 %put_out.1 = (bf16[5,512]{1,0:T(8,128)(2,1)}, bf16[448,512]{1,0:T(8,128)(2,1)}, bf16[448,512]{1,0:T(8,128)(2,1)}, bf16[448,512]{1,0:T(8,128)(2,1)}) custom-call(bf16[5,512]{1,0:T(8,128)(2,1)S(1)} %get-tuple-element.12.refs_0_, bf16[448,512]{1,0:T(8,128)(2,1)S(1)} %get-tuple-element.13.refs_1_, bf16[448,512]{1,0:T(8,128)(2,1)S(1)} %get-tuple-element.14.refs_2_, ...), custom_call_target="tpu_custom_call" | custom-call | tf_op jit(solution)/shard_map/put_out/pallas_call | solution.py:460
